TPU v7x, 32 devices: a whole 2x2x4 slice. The times are simulated.
32 devices in a mesh: seq: 8 (over y, x, core), batch: 4 (over z).
Axes of the slice: x: 2, y: 2, z: 4, core: 2. Of those that a mesh axis runs over, the one named last changes fastest.
Arguments:
- queries: bfloat16 [4096, 4096], P(('batch', 'seq')), parts along dimension 0, may hold values from -6 to 6
- key_vectors: bfloat16 [4096, 4096], P(('batch', 'seq')), parts along dimension 0, may hold values from -6 to 6
- value_vectors: bfloat16 [4096, 4096], P(('batch', 'seq')), parts along dimension 0, may hold values from -6 to 6
- residual_in: bfloat16 [4096, 4096], P(('batch', 'seq')), parts along dimension 0, may hold values from -6 to 6
- input_logit: float32 [8, 4096], P(None, ('batch', 'seq')), parts along dimension 1, may hold values from -8 to 300
- forget_logit: float32 [8, 4096], P(None, ('batch', 'seq')), parts along dimension 1, may hold values from -3 to 13
- mix_gain: float32 [4096], replicated, may hold values from 0.1 to 1.9
- ffn_gain: float32 [4096], replicated, may hold values from 0.1 to 1.9
- expert_gate: bfloat16 [8, 4096, 704], P('seq'), may hold values from -0.09375 to 0.09375
- expert_up: bfloat16 [8, 4096, 704], P('seq'), may hold values from -0.09375 to 0.09375
- expert_down: bfloat16 [8, 704, 4096], P('seq'), may hold values from -0.21875 to 0.21875
- routes: int32 [4096, 2], P(('batch', 'seq')), parts along dimension 0, may hold values from 0 to 7, all different within a row; in each aligned block of 128 rows (0 to 127, 128 to 255, ...) at most 64 rows name the same one
- route_weight: float32 [4096, 2], P(('batch', 'seq')), parts along dimension 0, may hold values from 0.2 to 1
Outputs:
- block_out: bfloat16 [4096, 4096], P(('batch', 'seq')), parts along dimension 0
There are 4 independent parts, one for each index of `batch`. A program takes and returns all parts, laid end to end along the dimension named above; an argument that names none is the same for every part. Nothing has to cross between parts.
Inputs may be any that keep to these rules, and one draw needn't show every extreme that they name: `routes`: each row names two different experts. Within the rows of one device no expert is named by more than 64 rows, and in some device one expert is named by exactly 64 rows.
All inputs are finite; a program needn't handle non-finite values.
Results may differ from a plain program's by a relative error of at most 0.0081.
Values may be sent and summed in bfloat16 or wider, within the bound.
No kernel may reach another device: no remote copies, remote signals or barrier semaphores. Data moves between devices by JAX's collectives and lax.ppermute only.
A program may use at most 128 MiB of HBM per device.

v0:
```python
import math
import jax
import jax.numpy as jnp
from jax import lax
from jax.sharding import PartitionSpec as P

NEG_FILL = -1e30
EPSILON = 1e-06


def join_states(earlier, later):
    total_early, state_early, normv_early, peak_early = earlier
    total_late, state_late, normv_late, peak_late = later
    carried = total_late + peak_early
    peak_new = jnp.maximum(carried, peak_late)
    scale_early = jnp.exp(carried - peak_new)
    scale_late = jnp.exp(peak_late - peak_new)
    state_new = scale_early[..., None] * state_early + scale_late[..., None] * state_late
    normv_new = scale_early * normv_early + scale_late * normv_late
    return (total_early + total_late, state_new, normv_new, peak_new)


def block_state(keys_three, values_three, log_forget, input_gate):
    cumul_log = jnp.cumsum(log_forget, axis=1)
    tail_log = cumul_log[:, -1:] - cumul_log + input_gate
    peak_tail = jnp.max(tail_log, axis=1)
    weight = jnp.exp(tail_log - peak_tail[:, None])
    weighted = keys_three.astype(jnp.float32) * jnp.transpose(weight)[:, :, None]
    rounded = weighted.astype(jnp.bfloat16)
    state_mat = jnp.einsum(
        "thd,the->hde", rounded, values_three, preferred_element_type=jnp.float32
    )
    norm_vec = jnp.sum(weighted, axis=0)
    return (
        jnp.broadcast_to(cumul_log[:, -1:], norm_vec.shape),
        state_mat,
        norm_vec,
        jnp.broadcast_to(peak_tail[:, None], norm_vec.shape),
    )


def block_mix(queries_three, keys_three, values_three, log_forget, input_gate, carry_in):
    tokens = queries_three.shape[0]
    inverse_root = 1.0 / math.sqrt(queries_three.shape[2])
    cumul_log = jnp.cumsum(log_forget, axis=1)
    carry_total, carry_state, carry_norm, carry_peak = carry_in
    log_weight = cumul_log[:, :, None] - cumul_log[:, None, :] + input_gate[:, None, :]
    causal = jnp.arange(tokens)[:, None] >= jnp.arange(tokens)[None, :]
    log_weight = jnp.where(causal[None], log_weight, NEG_FILL)
    carried = cumul_log + carry_peak[:, 0:1]
    peak_log = jnp.maximum(jnp.max(log_weight, axis=2), carried)
    decay_mat = jnp.exp(log_weight - peak_log[:, :, None])
    scores = (
        jnp.einsum("thd,shd->hts", queries_three, keys_three, preferred_element_type=jnp.float32)
        * inverse_root
    )
    coef = decay_mat * scores
    denom_sum = jnp.sum(coef, axis=2)
    numer_sum = jnp.einsum(
        "hts,she->the", coef.astype(jnp.bfloat16), values_three, preferred_element_type=jnp.float32
    )
    carry_reach = jnp.exp(carried - peak_log) * inverse_root
    query_float = queries_three.astype(jnp.float32)
    from_state = jnp.einsum(
        "thd,hde->the", query_float, carry_state, precision=lax.Precision.HIGHEST
    )
    from_norm = jnp.einsum("thd,hd->ht", query_float, carry_norm, precision=lax.Precision.HIGHEST)
    numer_sum = numer_sum + jnp.transpose(carry_reach)[:, :, None] * from_state
    denom_sum = denom_sum + carry_reach * from_norm
    floor_sum = jnp.maximum(jnp.abs(denom_sum), 1.0)
    return numer_sum / jnp.transpose(floor_sum)[:, :, None]


def shards(
    queries,
    key_vectors,
    value_vectors,
    residual_in,
    input_logit,
    forget_logit,
    mix_gain,
    ffn_gain,
    expert_gate,
    expert_up,
    expert_down,
    routes,
    route_weight,
):
    tokens, model_width = queries.shape
    head_count = input_logit.shape[0]
    head_dim = model_width // head_count
    devices = lax.axis_size("seq")
    queries_three = queries.reshape(tokens, head_count, head_dim)
    keys_three = key_vectors.reshape(tokens, head_count, head_dim)
    group = devices // head_count
    group_width = model_width // devices
    query_send = jnp.repeat(queries_three, group, axis=1)
    key_send = jnp.repeat(keys_three, group, axis=1)
    value_send = value_vectors.reshape(tokens, devices, group_width)
    query_all, key_all, value_all = (
        lax.all_to_all(query_send, "seq", split_axis=1, concat_axis=0, tiled=True),
        lax.all_to_all(key_send, "seq", split_axis=1, concat_axis=0, tiled=True),
        lax.all_to_all(value_send, "seq", split_axis=1, concat_axis=0, tiled=True),
    )
    input_all, forget_all = (
        lax.all_gather(input_logit, "seq", axis=1, tiled=True),
        lax.all_gather(forget_logit, "seq", axis=1, tiled=True),
    )
    head_index = lax.axis_index("seq") // group
    input_head = lax.dynamic_slice_in_dim(input_all, head_index, 1, 0)
    forget_head = jax.nn.log_sigmoid(lax.dynamic_slice_in_dim(forget_all, head_index, 1, 0))

    def per_block(array):
        return array.reshape((devices, tokens) + array.shape[1:])

    def per_gate(array):
        return jnp.transpose(array.reshape(1, devices, tokens), (1, 0, 2))

    start = (
        jnp.zeros((1, head_dim), jnp.float32),
        jnp.zeros((1, head_dim, group_width), jnp.float32),
        jnp.zeros((1, head_dim), jnp.float32),
        jnp.full((1, head_dim), NEG_FILL, jnp.float32),
    )

    def advance(carry_in, pieces):
        query_block, key_block, value_block, forget_block, input_block = pieces
        result = block_mix(query_block, key_block, value_block, forget_block, input_block, carry_in)
        carry_out = join_states(
            carry_in, block_state(key_block, value_block, forget_block, input_block)
        )
        return (carry_out, result)

    unused, mixed = lax.scan(
        advance,
        start,
        (
            per_block(query_all),
            per_block(key_all),
            per_block(value_all),
            per_gate(forget_head),
            per_gate(input_head),
        ),
    )
    mixed = mixed.reshape(devices * tokens, 1, group_width)
    mixer_out = lax.all_to_all(mixed, "seq", split_axis=0, concat_axis=1, tiled=True).reshape(
        tokens, model_width
    )
    mixer_square = jnp.mean(mixer_out * mixer_out, axis=1, keepdims=True)
    updated = (
        residual_in.astype(jnp.float32) + mixer_out * lax.rsqrt(mixer_square + EPSILON) * mix_gain
    ).astype(jnp.bfloat16)
    updated_float = updated.astype(jnp.float32)
    updated_square = jnp.mean(updated_float * updated_float, axis=1, keepdims=True)
    normed = (updated_float * lax.rsqrt(updated_square + EPSILON) * ffn_gain).astype(jnp.bfloat16)
    capacity = 4 * tokens // devices
    flat_routes = routes.reshape(-1)
    matches = (flat_routes[:, None] == jnp.arange(devices, dtype=jnp.int32)[None, :]).astype(
        jnp.int32
    )
    before = jnp.cumsum(matches, axis=0) - matches
    position = jnp.sum(before * matches, axis=1)
    slot_index = (flat_routes * capacity + position).reshape(tokens, 2)
    columns = jnp.arange(devices * capacity, dtype=jnp.int32)
    pick_first = (slot_index[:, 0:1] == columns[None, :]).astype(jnp.bfloat16)
    pick_second = (slot_index[:, 1:2] == columns[None, :]).astype(jnp.bfloat16)
    spread = jnp.einsum(
        "tc,td->cd", pick_first + pick_second, normed, preferred_element_type=jnp.float32
    ).astype(jnp.bfloat16)
    outbound = spread.reshape(devices, capacity, model_width)
    block_in = lax.all_to_all(outbound, "seq", split_axis=0, concat_axis=0, tiled=True)
    row_block = block_in.reshape(-1, model_width)
    gate_val = jnp.dot(row_block, expert_gate[0], preferred_element_type=jnp.float32)
    up_val = jnp.dot(row_block, expert_up[0], preferred_element_type=jnp.float32)
    hidden = (jax.nn.silu(gate_val) * up_val).astype(jnp.bfloat16)
    result = jnp.dot(hidden, expert_down[0], preferred_element_type=jnp.float32).astype(
        jnp.bfloat16
    )
    inbound = lax.all_to_all(
        result.reshape(block_in.shape), "seq", split_axis=0, concat_axis=0, tiled=True
    )
    flat_back = inbound.reshape(devices * capacity, model_width)
    first_out = jnp.dot(pick_first, flat_back, preferred_element_type=jnp.float32)
    second_out = jnp.dot(pick_second, flat_back, preferred_element_type=jnp.float32)
    expert_mix = route_weight[:, 0:1] * first_out + route_weight[:, 1:2] * second_out
    return (updated_float + expert_mix).astype(jnp.bfloat16)


def solution(mesh):
    return jax.shard_map(
        shards,
        mesh=mesh,
        in_specs=(
            P(("batch", "seq"), None),
            P(("batch", "seq"), None),
            P(("batch", "seq"), None),
            P(("batch", "seq"), None),
            P(None, ("batch", "seq")),
            P(None, ("batch", "seq")),
            P(),
            P(),
            P("seq", None, None),
            P("seq", None, None),
            P("seq", None, None),
            P(("batch", "seq"), None),
            P(("batch", "seq"), None),
        ),
        out_specs=P(("batch", "seq"), None),
        check_vma=False,
    )
```

profile of v0, /device:TPU:0, one launch (start us, length us, event | category | flops | bytes accessed | tf_op | source)
XLA Modules:
  0.0 361.2 jit_solution(481874486688636953)
XLA Ops:
  0.0 2.3 copy.82
  2.3 5.2 %all-to-all-start = ((bf16[128,8,512]{0,2,1:T(8,128)(2,1)}), bf16[128,8,512]{0,2,1:T(8,128)(2,1)S(1)}, u32[]{:S(2)}, u32[]{:S(2)}) async-start(bf16[128,8,512]{0,2,1:T(8,128)(2,1)} %bitcast.2), calls=%async_computation | async-start | bytes 2097152 | tf_op jit(solution)/shard_map/all_to_all | solution.py:102
  7.6 1.3 copy.84
  8.9 14.1 %all-to-all-done = bf16[128,8,512]{0,2,1:T(8,128)(2,1)S(1)} async-done(((bf16[128,8,512]{0,2,1:T(8,128)(2,1)}), bf16[128,8,512]{0,2,1:T(8,128)(2,1)S(1)}, u32[]{:S(2)}, u32[]{:S(2)}) %all-to-all-start) | async-done | bytes 1048608 | tf_op jit(solution)/shard_map/all_to_all | solution.py:102
  22.9 3.6 all-to-all-start.1
  26.5 1.3 copy.86
  27.8 14.0 %all-to-all-done.1 = bf16[128,8,512]{0,2,1:T(8,128)(2,1)S(1)} async-done(((bf16[128,8,512]{0,2,1:T(8,128)(2,1)}), bf16[128,8,512]{0,2,1:T(8,128)(2,1)S(1)}, u32[]{:S(2)}, u32[]{:S(2)}) %all-to-all-start.1) | async-done | bytes 1048608 | tf_op jit(solution)/shard_map/all_to_all | solution.py:103
  41.8 4.2 %all-to-all-start.2 = ((bf16[128,8,512]{0,2,1:T(8,128)(2,1)}), bf16[128,8,512]{0,2,1:T(8,128)(2,1)}, u32[]{:S(2)}, u32[]{:S(2)}) async-start(bf16[128,8,512]{0,2,1:T(8,128)(2,1)} %bitcast.8), calls=%async_computation.2 | async-start | bytes 2097152 | tf_op jit(solution)/shard_map/all_to_all | solution.py:101
  46.1 18.5 %all_gather.7 = f32[8,1024]{1,0:T(8,128)S(1)} all-gather(f32[8,128]{1,0:T(8,128)S(1)} %copy-done.9), channel_id=1, replica_groups=mesh['seq'=8,'batch'=4] {'seq'}, dimensions={1}, use_global_device_ids=true | all-gather | bytes 36864 | tf_op jit(solution)/shard_map/all_gather | solution.py:106
  64.6 8.2 %all_gather.6 = f32[8,1024]{1,0:T(8,128)S(1)} all-gather(f32[8,128]{1,0:T(8,128)S(1)} %copy-done.10), channel_id=1, replica_groups=mesh['seq'=8,'batch'=4] {'seq'}, dimensions={1}, use_global_device_ids=true | all-gather | bytes 36864 | tf_op jit(solution)/shard_map/all_gather | solution.py:107
  72.8 1.7 copy.83
  74.5 1.5 copy.88
  76.1 1.7 copy.85
  77.8 1.5 copy.89
  79.3 2.7 copy.87
  82.0 2.5 copy.90
  84.5 105.7 %while.17 = (s32[]{:T(128)}, f32[1,512,512]{2,1,0:T(8,128)S(1)}, f32[1,512]{1,0:T(1,128)S(1)}, f32[1,512]{1,0:T(1,128)S(1)}, f32[8,128,1,512]{3,1,0,2:T(8,128)},...) while((s32[]{:T(128)}, f32[1,512,512]{2,1,0:T(8,128)S(1)}, ...), condition=%wide.region_6.7_spmd.clone, body=%wide.region_0.6_spmd.clone.sunk | while | flops 506255232 | bytes 14530822 | solution.py:134
  85.5 1.3 fusion.115
  86.8 1.3 subtract_exponential_fusion.6
  88.1 1.3 multiply_add_fusion.3
  93.3 2.0 fusion.120
  96.1 1.5 fusion.117
  98.7 1.3 fusion.115
  100.0 1.3 subtract_exponential_fusion.6
  101.3 1.3 multiply_add_fusion.3
  106.5 2.0 fusion.120
  109.3 1.5 fusion.117
  111.9 1.3 fusion.115
  114.6 1.3 multiply_add_fusion.3
  119.7 2.0 fusion.120
  122.5 1.5 fusion.117
  125.1 1.3 fusion.115
  127.8 1.3 multiply_add_fusion.3
  132.9 2.0 fusion.120
  135.8 1.5 fusion.117
  138.3 1.3 fusion.115
  139.6 1.3 subtract_exponential_fusion.6
  141.0 1.3 multiply_add_fusion.3
  146.1 2.0 fusion.120
  149.0 1.5 fusion.117
  151.5 1.3 fusion.115
  154.2 1.3 multiply_add_fusion.3
  159.4 2.0 fusion.120
  162.2 1.5 fusion.117
  164.8 1.3 fusion.115
  167.4 1.3 multiply_add_fusion.3
  172.6 2.0 fusion.120
  175.5 1.5 fusion.117
  178.0 1.3 fusion.115
  180.7 1.3 multiply_add_fusion.3
  185.8 2.0 fusion.120
  188.7 1.5 fusion.117
  190.2 5.0 %copy.92 = f32[1024,1,512]{2,1,0:T(1,128)} copy(f32[1024,1,512]{2,0,1:T(8,128)} %bitcast.226) | data formatting | bytes 4194304 | tf_op jit(solution)/shard_map/reshape | solution.py:145
  195.2 3.9 %all-to-all-start.3 = ((f32[1024,1,512]{2,1,0:T(1,128)}), f32[1024,1,512]{2,1,0:T(1,128)S(1)}, u32[]{:S(2)}, u32[]{:S(2)}) async-start(f32[1024,1,512]{2,1,0:T(1,128)} %copy.92), calls=%async_computation.3 | async-start | bytes 4194304 | tf_op jit(solution)/shard_map/all_to_all | solution.py:146
  200.7 24.8 %all-to-all-done.3 = f32[1024,1,512]{2,1,0:T(1,128)S(1)} async-done(((f32[1024,1,512]{2,1,0:T(1,128)}), f32[1024,1,512]{2,1,0:T(1,128)S(1)}, u32[]{:S(2)}, u32[]{:S(2)}) %all-to-all-start.3) | async-done | bytes 2097184 | tf_op jit(solution)/shard_map/all_to_all | solution.py:146
  227.9 1.4 convolution_convert_fusion
  229.3 51.7 %all_to_all.70 = bf16[8,64,4096]{2,1,0:T(8,128)(2,1)S(1)} all-to-all(bf16[8,64,4096]{2,1,0:T(8,128)(2,1)S(1)} %bitcast.216), channel_id=1, replica_groups=mesh['seq'=8,'batch'=4] {'seq'}, dimensions={0} | all-to-all | bytes 8388608 | tf_op jit(solution)/shard_map/all_to_all | solution.py:171
  281.0 2.0 copy-done.2
  282.9 3.2 fusion.50
  286.1 14.1 %convolution_convert_fusion.1 = bf16[512,4096]{1,0:T(8,128)(2,1)} fusion(bf16[1,704,4096]{2,1,0:T(8,128)(2,1)} %param.25, bf16[512,4096]{1,0:T(8,128)(2,1)} %bitcast.222, bf16[1,4096,704]{1,2,0:T(8,128)(2,1)} %param.24, f32[512,704]{0,1:T(8,128)S(1)} %fusion.50), kind=kOutput, calls=%fused_computation.70 | convolution fusion | flops 5909839872 | bytes 21364736 | tf_op jit(solution)/shard_map/dot_general | solution.py:176
  300.2 4.7 %all-to-all-start.5 = ((bf16[8,64,4096]{2,1,0:T(8,128)(2,1)}), bf16[8,64,4096]{2,1,0:T(8,128)(2,1)}, u32[]{:S(2)}, u32[]{:S(2)}) async-start(bf16[8,64,4096]{2,1,0:T(8,128)(2,1)} %bitcast.220), calls=%async_computation.5 | async-start | bytes 8388608 | tf_op jit(solution)/shard_map/all_to_all | solution.py:179
  304.9 49.1 %all-to-all-done.5 = bf16[8,64,4096]{2,1,0:T(8,128)(2,1)} async-done(((bf16[8,64,4096]{2,1,0:T(8,128)(2,1)}), bf16[8,64,4096]{2,1,0:T(8,128)(2,1)}, u32[]{:S(2)}, u32[]{:S(2)}) %all-to-all-start.5) | async-done | bytes 4194336 | tf_op jit(solution)/shard_map/all_to_all | solution.py:179
  354.0 2.9 convolution_multiply_fusion.3
  356.9 4.2 %fusion.54 = bf16[128,4096]{1,0:T(8,128)(2,1)} fusion(f32[128,4096]{1,0:T(8,128)S(1)} %convolution_multiply_fusion.3, bf16[512,4096]{1,0:T(8,128)(2,1)} %bitcast.24, bf16[128,4096]{1,0:T(8,128)(2,1)S(1)} %get-tuple-element.169, f32[128]{0:T(128)S(1)} %get-tuple-element.174, s32[128]{0:T(128)S(1)} %get-tuple-element.177), kind=kOutput, calls=%fused_computation.80 | convolution fusion | flops 539557888 | bytes 8389632 | tf_op jit(solution)/shard_map/dot_general | solution.py:184
  (192 shorter events, 56.8 us)
Async XLA Ops:
  0.0 7.6 %copy-start.4 = (bf16[128,4096]{1,0:T(8,128)(2,1)S(1)}, bf16[128,4096]{1,0:T(8,128)(2,1)}, u32[]{:S(2)}) copy-start(bf16[128,4096]{1,0:T(8,128)(2,1)} %param.17) | copy-start | bytes 3145732
  2.3 20.6 %all-to-all-start = ((bf16[128,8,512]{0,2,1:T(8,128)(2,1)}), bf16[128,8,512]{0,2,1:T(8,128)(2,1)S(1)}, u32[]{:S(2)}, u32[]{:S(2)}) async-start(bf16[128,8,512]{0,2,1:T(8,128)(2,1)} %bitcast.2), calls=%async_computation | async-start | bytes 2097152 | tf_op jit(solution)/shard_map/all_to_all | solution.py:102
  8.9 17.6 %copy-start.5 = (bf16[128,4096]{1,0:T(8,128)(2,1)S(1)}, bf16[128,4096]{1,0:T(8,128)(2,1)}, u32[]{:S(2)}) copy-start(bf16[128,4096]{1,0:T(8,128)(2,1)} %param.15) | copy-start | bytes 3145732
  22.9 18.9 %all-to-all-start.1 = ((bf16[128,8,512]{0,2,1:T(8,128)(2,1)}), bf16[128,8,512]{0,2,1:T(8,128)(2,1)S(1)}, u32[]{:S(2)}, u32[]{:S(2)}) async-start(bf16[128,8,512]{0,2,1:T(8,128)(2,1)} %bitcast.5), calls=%async_computation.1 | async-start | bytes 2097152 | tf_op jit(solution)/shard_map/all_to_all | solution.py:103
  26.5 19.6 %copy-start.9 = (f32[8,128]{1,0:T(8,128)S(1)}, f32[8,128]{1,0:T(8,128)}, u32[]{:S(2)}) copy-start(f32[8,128]{1,0:T(8,128)} %param.19) | copy-start | bytes 12292
  26.5 38.1 %copy-start.10 = (f32[8,128]{1,0:T(8,128)S(1)}, f32[8,128]{1,0:T(8,128)}, u32[]{:S(2)}) copy-start(f32[8,128]{1,0:T(8,128)} %param.20) | copy-start | bytes 12292
  41.8 37.5 %all-to-all-start.2 = ((bf16[128,8,512]{0,2,1:T(8,128)(2,1)}), bf16[128,8,512]{0,2,1:T(8,128)(2,1)}, u32[]{:S(2)}, u32[]{:S(2)}) async-start(bf16[128,8,512]{0,2,1:T(8,128)(2,1)} %bitcast.8), calls=%async_computation.2 | async-start | bytes 2097152 | tf_op jit(solution)/shard_map/all_to_all | solution.py:101
  84.5 8.8 %copy-start = (bf16[8,128,1,512]{3,1,2,0:T(8,128)(2,1)}, bf16[8,128,1,512]{3,1,2,0:T(8,128)(2,1)S(1)}, u32[]{:S(2)}) copy-start(bf16[8,128,1,512]{3,1,2,0:T(8,128)(2,1)S(1)} %get-tuple-element.297) | copy-start | bytes 3145732 | tf_op jit(solution)/shard_map/while
  96.1 1.5 copy-start.1
  97.7 8.8 %copy-start = (bf16[8,128,1,512]{3,1,2,0:T(8,128)(2,1)}, bf16[8,128,1,512]{3,1,2,0:T(8,128)(2,1)S(1)}, u32[]{:S(2)}) copy-start(bf16[8,128,1,512]{3,1,2,0:T(8,128)(2,1)S(1)} %get-tuple-element.297) | copy-start | bytes 3145732 | tf_op jit(solution)/shard_map/while
  109.3 1.5 copy-start.1
  110.9 8.8 %copy-start = (bf16[8,128,1,512]{3,1,2,0:T(8,128)(2,1)}, bf16[8,128,1,512]{3,1,2,0:T(8,128)(2,1)S(1)}, u32[]{:S(2)}) copy-start(bf16[8,128,1,512]{3,1,2,0:T(8,128)(2,1)S(1)} %get-tuple-element.297) | copy-start | bytes 3145732 | tf_op jit(solution)/shard_map/while
  122.5 1.5 copy-start.1
  124.1 8.8 %copy-start = (bf16[8,128,1,512]{3,1,2,0:T(8,128)(2,1)}, bf16[8,128,1,512]{3,1,2,0:T(8,128)(2,1)S(1)}, u32[]{:S(2)}) copy-start(bf16[8,128,1,512]{3,1,2,0:T(8,128)(2,1)S(1)} %get-tuple-element.297) | copy-start | bytes 3145732 | tf_op jit(solution)/shard_map/while
  135.8 1.5 copy-start.1
  137.3 8.9 %copy-start = (bf16[8,128,1,512]{3,1,2,0:T(8,128)(2,1)}, bf16[8,128,1,512]{3,1,2,0:T(8,128)(2,1)S(1)}, u32[]{:S(2)}) copy-start(bf16[8,128,1,512]{3,1,2,0:T(8,128)(2,1)S(1)} %get-tuple-element.297) | copy-start | bytes 3145732 | tf_op jit(solution)/shard_map/while
  149.0 1.5 copy-start.1
  150.5 8.8 %copy-start = (bf16[8,128,1,512]{3,1,2,0:T(8,128)(2,1)}, bf16[8,128,1,512]{3,1,2,0:T(8,128)(2,1)S(1)}, u32[]{:S(2)}) copy-start(bf16[8,128,1,512]{3,1,2,0:T(8,128)(2,1)S(1)} %get-tuple-element.297) | copy-start | bytes 3145732 | tf_op jit(solution)/shard_map/while
  162.2 1.5 copy-start.1
  163.8 8.8 %copy-start = (bf16[8,128,1,512]{3,1,2,0:T(8,128)(2,1)}, bf16[8,128,1,512]{3,1,2,0:T(8,128)(2,1)S(1)}, u32[]{:S(2)}) copy-start(bf16[8,128,1,512]{3,1,2,0:T(8,128)(2,1)S(1)} %get-tuple-element.297) | copy-start | bytes 3145732 | tf_op jit(solution)/shard_map/while
  175.4 1.5 copy-start.1
  177.0 8.8 %copy-start = (bf16[8,128,1,512]{3,1,2,0:T(8,128)(2,1)}, bf16[8,128,1,512]{3,1,2,0:T(8,128)(2,1)S(1)}, u32[]{:S(2)}) copy-start(bf16[8,128,1,512]{3,1,2,0:T(8,128)(2,1)S(1)} %get-tuple-element.297) | copy-start | bytes 3145732 | tf_op jit(solution)/shard_map/while
  188.7 1.5 copy-start.1
  195.2 3.9 %copy-start.8 = (s32[128,2]{0,1:T(2,128)S(1)}, s32[128,2]{0,1:T(2,128)}, u32[]{:S(2)}) copy-start(s32[128,2]{0,1:T(2,128)} %param.26) | copy-start | bytes 3076
  195.2 30.3 %all-to-all-start.3 = ((f32[1024,1,512]{2,1,0:T(1,128)}), f32[1024,1,512]{2,1,0:T(1,128)S(1)}, u32[]{:S(2)}, u32[]{:S(2)}) async-start(f32[1024,1,512]{2,1,0:T(1,128)} %copy.92), calls=%async_computation.3 | async-start | bytes 4194304 | tf_op jit(solution)/shard_map/all_to_all | solution.py:146
  225.9 1.2 copy-start.3
  226.0 1.2 copy-start.6
  227.2 0.7 copy-start.7
  227.9 55.0 %slice-start = ((s8[5767168]{0:T(1024)(128)(4,1)}), s8[4194304]{0:T(1024)(128)(4,1)S(1)}, s32[]{:S(2)}) async-start(s8[5767168]{0:T(1024)(128)(4,1)} %bitcast.232), calls=%async_computation.6 | async-start | bytes 8388608
  229.3 53.6 %slice-start.1 = ((s8[5767168]{0:T(1024)(128)(4,1)}), s8[1572864]{0:T(1024)(128)(4,1)S(1)}, s32[]{:S(2)}) async-start(s8[5767168]{0:T(1024)(128)(4,1)} %bitcast.232), calls=%async_computation.7 | async-start | bytes 3145728
  281.0 2.0 copy-start.2
  300.2 4.7 %copy-start.11 = (f32[128,2]{0,1:T(2,128)S(1)}, f32[128,2]{0,1:T(2,128)}, u32[]{:S(2)}) copy-start(f32[128,2]{0,1:T(2,128)} %param.27) | copy-start | bytes 3076
  300.2 53.8 %all-to-all-start.5 = ((bf16[8,64,4096]{2,1,0:T(8,128)(2,1)}), bf16[8,64,4096]{2,1,0:T(8,128)(2,1)}, u32[]{:S(2)}, u32[]{:S(2)}) async-start(bf16[8,64,4096]{2,1,0:T(8,128)(2,1)} %bitcast.220), calls=%async_computation.5 | async-start | bytes 8388608 | tf_op jit(solution)/shard_map/all_to_all | solution.py:179
where the time goes:
time: 363 us; the launch traced here: 361 us
  waiting for transfers between devices  102 us (28%)
  blocking collectives  78.4 us (22%)
  matrix products  72.6 us (20%)
  local copies, waits for them, and re-layouts  42.9 us (12%)
  other arithmetic  42.8 us (12%)
  starting transfers between devices  21.6 us (6%)
    all_to_all x1, blocking collectives, shards(): lax.all_to_all(outbound, 'seq', split_axis=0, concat_axis=0, tiled=True)  51.7 us
    all_to_all x1, waiting for transfers between devices, shards(): lax.all_to_all(result.reshape(block_in.shape), 'seq', split_axis=0, conca...  49.1 us
    all_to_all x1, waiting for transfers between devices, shards(): lax.all_to_all(mixed, 'seq', split_axis=0, concat_axis=1, tiled=True)  24.8 us
    all_gather x1, blocking collectives, shards(): lax.all_gather(input_logit, 'seq', axis=1, tiled=True)  18.5 us
    dot_general x8, matrix products, block_mix(): jnp.einsum('thd,hde->the', query_float, carry_state, precision=lax.Precis...  15.8 us
    dot_general x1, matrix products, shards(): jnp.dot(hidden, expert_down[0], preferred_element_type=jnp.float32)  14.1 us
    unnamed x33, local copies, waits for them, and re-layouts  14.1 us
    all_to_all x1, waiting for transfers between devices, shards(): lax.all_to_all(key_send, 'seq', split_axis=1, concat_axis=0, tiled=True)  14.1 us
  transfers between devices with their start and end apart: 5, of which 4 were waited for; matrix products, arithmetic and copies ran while one was open for 3% of the time, Pallas kernels for 0%

commit v1 on v0

--- a/solution.py
+++ b/solution.py
@@ -168,7 +168,15 @@
         "tc,td->cd", pick_first + pick_second, normed, preferred_element_type=jnp.float32
     ).astype(jnp.bfloat16)
     outbound = spread.reshape(devices, capacity, model_width)
-    block_in = lax.all_to_all(outbound, "seq", split_axis=0, concat_axis=0, tiled=True)
+    ways, here = (lax.axis_size("seq"), lax.axis_index("seq"))
+    width = outbound.shape[0] // ways
+    turned = jnp.roll(outbound, -here * width, axis=0)
+    got = [lax.slice_in_dim(turned, 0, width, axis=0)]
+    for far in range(1, ways):
+        sent = lax.slice_in_dim(turned, far * width, (far + 1) * width, axis=0)
+        got.append(lax.ppermute(sent, "seq", [(d, (d + far) % ways) for d in range(ways)]))
+    line = jnp.concatenate(got[::-1], axis=0)
+    block_in = jnp.roll(line, (here + 1) * got[0].shape[0], axis=0)
     row_block = block_in.reshape(-1, model_width)
     gate_val = jnp.dot(row_block, expert_gate[0], preferred_element_type=jnp.float32)
     up_val = jnp.dot(row_block, expert_up[0], preferred_element_type=jnp.float32)

time: 363 us -> 369 us (1.017)
  blocking collectives: 78.4 us -> 26.7 us
  waiting for transfers between devices: 102 us -> 144 us
  matrix products: 72.6 us -> 79 us
  local copies, waits for them, and re-layouts: 42.9 us -> 48 us
    all_to_all x1 -> x0, blocking collectives: 51.7 us -> none  [shards(): lax.all_to_all(outbound, 'seq', split_axis=0, concat_axis=0, tiled=True)]
    ppermute x0 -> x7, waiting for transfers between devices: none -> 43.5 us  [shards(): lax.ppermute(sent, 'seq', [(d, (d + far) % ways) for d in range(ways)])]
    dot_general x8, matrix products: 1.7 us -> 8.9 us  [block_mix(): jnp.einsum('hts,she->the', coef.astype(jnp.bfloat16), values_three, prefe...]
    unnamed x33 -> x40, local copies, waits for them, and re-layouts: 14.1 us -> 18.8 us
  transfers between devices with their start and end apart: 5 -> 12, of which waited for: 4 -> 9; matrix products, arithmetic and copies ran while one was open for 3% -> 4% of each run, Pallas kernels for 0% -> 0%
where the time goes in v1:
time: 369 us; the launch traced here: 367 us
  waiting for transfers between devices  144 us (39%)
  matrix products  79 us (21%)
  local copies, waits for them, and re-layouts  48 us (13%)
  other arithmetic  42.9 us (12%)
  blocking collectives  26.7 us (7%)
  starting transfers between devices  24.9 us (7%)
    all_to_all x1, waiting for transfers between devices, shards(): lax.all_to_all(result.reshape(block_in.shape), 'seq', split_axis=0, conca...  49.1 us
    ppermute x7, waiting for transfers between devices, shards(): lax.ppermute(sent, 'seq', [(d, (d + far) % ways) for d in range(ways)])  43.5 us
    all_to_all x1, waiting for transfers between devices, shards(): lax.all_to_all(mixed, 'seq', split_axis=0, concat_axis=1, tiled=True)  24.7 us
    unnamed x40, local copies, waits for them, and re-layouts  18.8 us
    all_gather x1, blocking collectives, shards(): lax.all_gather(input_logit, 'seq', axis=1, tiled=True)  18.5 us
    dot_general x8, matrix products, block_mix(): jnp.einsum('thd,hde->the', query_float, carry_state, precision=lax.Precis...  15.8 us
    dot_general x1, matrix products, shards(): jnp.dot(hidden, expert_down[0], preferred_element_type=jnp.float32)  14.1 us
    all_to_all x1, waiting for transfers between devices, shards(): lax.all_to_all(key_send, 'seq', split_axis=1, concat_axis=0, tiled=True)  14 us
  transfers between devices with their start and end apart: 12, of which 9 were waited for; matrix products, arithmetic and copies ran while one was open for 4% of the time, Pallas kernels for 0%

profile of v1, /device:TPU:0, one launch (start us, length us, event | category | flops | bytes accessed | tf_op | source)
XLA Modules:
  0.0 367.0 jit_solution(16989798288383947038)
XLA Ops:
  0.0 2.3 copy.82
  2.3 5.2 %all-to-all-start = ((bf16[128,8,512]{0,2,1:T(8,128)(2,1)}), bf16[128,8,512]{0,2,1:T(8,128)(2,1)S(1)}, u32[]{:S(2)}, u32[]{:S(2)}) async-start(bf16[128,8,512]{0,2,1:T(8,128)(2,1)} %bitcast.2), calls=%async_computation | async-start | bytes 2097152 | tf_op jit(solution)/shard_map/all_to_all | solution.py:102
  7.6 1.3 copy.84
  8.9 14.0 %all-to-all-done = bf16[128,8,512]{0,2,1:T(8,128)(2,1)S(1)} async-done(((bf16[128,8,512]{0,2,1:T(8,128)(2,1)}), bf16[128,8,512]{0,2,1:T(8,128)(2,1)S(1)}, u32[]{:S(2)}, u32[]{:S(2)}) %all-to-all-start) | async-done | bytes 1048608 | tf_op jit(solution)/shard_map/all_to_all | solution.py:102
  22.9 3.6 all-to-all-start.1
  26.5 2.3 copy.86
  28.7 13.1 %all-to-all-done.1 = bf16[128,8,512]{0,2,1:T(8,128)(2,1)S(1)} async-done(((bf16[128,8,512]{0,2,1:T(8,128)(2,1)}), bf16[128,8,512]{0,2,1:T(8,128)(2,1)S(1)}, u32[]{:S(2)}, u32[]{:S(2)}) %all-to-all-start.1) | async-done | bytes 1048608 | tf_op jit(solution)/shard_map/all_to_all | solution.py:103
  41.8 4.2 %all-to-all-start.2 = ((bf16[128,8,512]{0,2,1:T(8,128)(2,1)}), bf16[128,8,512]{0,2,1:T(8,128)(2,1)}, u32[]{:S(2)}, u32[]{:S(2)}) async-start(bf16[128,8,512]{0,2,1:T(8,128)(2,1)} %bitcast.8), calls=%async_computation.2 | async-start | bytes 2097152 | tf_op jit(solution)/shard_map/all_to_all | solution.py:101
  46.1 18.5 %all_gather.7 = f32[8,1024]{1,0:T(8,128)S(1)} all-gather(f32[8,128]{1,0:T(8,128)S(1)} %copy-done.7), channel_id=1, replica_groups=mesh['seq'=8,'batch'=4] {'seq'}, dimensions={1}, use_global_device_ids=true | all-gather | bytes 36864 | tf_op jit(solution)/shard_map/all_gather | solution.py:106
  64.6 8.2 %all_gather.6 = f32[8,1024]{1,0:T(8,128)S(1)} all-gather(f32[8,128]{1,0:T(8,128)S(1)} %copy-done.8), channel_id=1, replica_groups=mesh['seq'=8,'batch'=4] {'seq'}, dimensions={1}, use_global_device_ids=true | all-gather | bytes 36864 | tf_op jit(solution)/shard_map/all_gather | solution.py:107
  72.8 1.7 copy.83
  74.5 1.5 copy.88
  76.1 1.7 copy.85
  77.7 2.5 copy.89
  80.3 1.9 copy.87
  82.1 1.3 copy.90
  83.4 107.7 %while.17 = (s32[]{:T(128)}, f32[1,512,512]{2,1,0:T(8,128)S(1)}, f32[1,512]{1,0:T(1,128)S(1)}, f32[1,512]{1,0:T(1,128)S(1)}, f32[8,128,1,512]{3,1,0,2:T(8,128)},...) while((s32[]{:T(128)}, f32[1,512,512]{2,1,0:T(8,128)S(1)}, ...), condition=%wide.region_6.7_spmd.clone, body=%wide.region_0.6_spmd.clone.sunk | while | flops 506255232 | bytes 6142666 | solution.py:134
  85.5 1.2 subtract_exponential_fusion.6
  86.8 1.2 multiply_add_fusion.3
  92.6 2.0 fusion.123
  95.5 1.4 fusion.120
  100.3 1.2 multiply_add_fusion.3
  106.1 2.0 fusion.123
  108.9 1.4 fusion.120
  112.4 1.2 subtract_exponential_fusion.6
  113.8 1.2 multiply_add_fusion.3
  119.5 2.0 fusion.123
  122.4 1.4 fusion.120
  127.2 1.2 multiply_add_fusion.3
  133.0 2.0 fusion.123
  135.8 1.4 fusion.120
  140.7 1.2 multiply_add_fusion.3
  146.5 2.0 fusion.123
  149.3 1.4 fusion.120
  154.1 1.2 multiply_add_fusion.3
  159.9 2.0 fusion.123
  162.8 1.4 fusion.120
  167.6 1.2 multiply_add_fusion.3
  173.4 2.0 fusion.123
  176.2 1.4 fusion.120
  181.1 1.2 multiply_add_fusion.3
  186.8 2.0 fusion.123
  189.7 1.4 fusion.120
  191.1 5.1 %copy.92 = f32[1024,1,512]{2,1,0:T(1,128)} copy(f32[1024,1,512]{2,0,1:T(8,128)} %bitcast.226) | data formatting | bytes 4194304 | tf_op jit(solution)/shard_map/reshape | solution.py:145
  196.2 3.8 %all-to-all-start.3 = ((f32[1024,1,512]{2,1,0:T(1,128)}), f32[1024,1,512]{2,1,0:T(1,128)S(1)}, u32[]{:S(2)}, u32[]{:S(2)}) async-start(f32[1024,1,512]{2,1,0:T(1,128)} %copy.92), calls=%async_computation.3 | async-start | bytes 4194304 | tf_op jit(solution)/shard_map/all_to_all | solution.py:146
  201.6 24.7 %all-to-all-done.3 = f32[1024,1,512]{2,1,0:T(1,128)S(1)} async-done(((f32[1024,1,512]{2,1,0:T(1,128)}), f32[1024,1,512]{2,1,0:T(1,128)S(1)}, u32[]{:S(2)}, u32[]{:S(2)}) %all-to-all-start.3) | async-done | bytes 2097184 | tf_op jit(solution)/shard_map/all_to_all | solution.py:146
  228.4 1.4 convolution_convert_fusion
  229.8 1.6 fusion.56
  231.4 1.9 copy-done
  233.3 1.3 fusion.88
  235.2 1.2 collective-permute-start.2
  238.1 9.2 %collective-permute-done = bf16[1,64,4096]{2,1,0:T(8,128)(2,1)} collective-permute-done((bf16[1,64,4096]{2,1,0:T(8,128)(2,1)}, bf16[1,64,4096]{2,1,0:T(8,128)(2,1)}, u32[]{:S(2)}, u32[]{:S(2)}) %collective-permute-start) | collective-permute-done | bytes 524320 | tf_op jit(solution)/shard_map/ppermute | solution.py:177
  248.3 10.2 %collective-permute-done.1 = bf16[1,64,4096]{2,1,0:T(8,128)(2,1)} collective-permute-done((bf16[1,64,4096]{2,1,0:T(8,128)(2,1)}, bf16[1,64,4096]{2,1,0:T(8,128)(2,1)}, u32[]{:S(2)}, u32[]{:S(2)}) %collective-permute-start.1) | collective-permute-done | bytes 524320 | tf_op jit(solution)/shard_map/ppermute | solution.py:177
  260.5 21.7 %collective-permute-done.3 = bf16[1,64,4096]{2,1,0:T(8,128)(2,1)S(1)} collective-permute-done((bf16[1,64,4096]{2,1,0:T(8,128)(2,1)S(1)}, bf16[1,64,4096]{2,1,0:T(8,128)(2,1)S(1)}, u32[]{:S(2)}, u32[]{:S(2)}) %collective-permute-start.3) | collective-permute-done | bytes 524320 | tf_op jit(solution)/shard_map/ppermute | solution.py:177
  282.2 1.6 collective-permute-done.4
  283.9 1.2 slice_dynamic-update-slice_fusion
  285.2 1.6 fusion.55
  286.8 2.0 copy-done.1
  288.8 3.2 fusion.50
  291.9 14.1 %convolution_convert_fusion.1 = bf16[512,4096]{1,0:T(8,128)(2,1)} fusion(bf16[1,704,4096]{2,1,0:T(8,128)(2,1)} %param.27, bf16[512,4096]{1,0:T(8,128)(2,1)} %bitcast.222, bf16[1,4096,704]{1,2,0:T(8,128)(2,1)} %param.26, f32[512,704]{0,1:T(8,128)S(1)} %fusion.50), kind=kOutput, calls=%fused_computation.74 | convolution fusion | flops 5909839872 | bytes 21364736 | tf_op jit(solution)/shard_map/dot_general | solution.py:184
  306.0 4.7 %all-to-all-start.4 = ((bf16[8,64,4096]{2,1,0:T(8,128)(2,1)}), bf16[8,64,4096]{2,1,0:T(8,128)(2,1)}, u32[]{:S(2)}, u32[]{:S(2)}) async-start(bf16[8,64,4096]{2,1,0:T(8,128)(2,1)} %bitcast.220), calls=%async_computation.4 | async-start | bytes 8388608 | tf_op jit(solution)/shard_map/all_to_all | solution.py:187
  310.7 49.1 %all-to-all-done.4 = bf16[8,64,4096]{2,1,0:T(8,128)(2,1)} async-done(((bf16[8,64,4096]{2,1,0:T(8,128)(2,1)}), bf16[8,64,4096]{2,1,0:T(8,128)(2,1)}, u32[]{:S(2)}, u32[]{:S(2)}) %all-to-all-start.4) | async-done | bytes 4194336 | tf_op jit(solution)/shard_map/all_to_all | solution.py:187
  359.8 2.9 convolution_multiply_fusion.3
  362.7 4.3 %fusion.54 = bf16[128,4096]{1,0:T(8,128)(2,1)} fusion(f32[128,4096]{1,0:T(8,128)S(1)} %convolution_multiply_fusion.3, bf16[512,4096]{1,0:T(8,128)(2,1)} %bitcast.24, bf16[128,4096]{1,0:T(8,128)(2,1)S(1)} %get-tuple-element.170, f32[128]{0:T(128)S(1)} %get-tuple-element.182, s32[128]{0:T(128)S(1)} %get-tuple-element.185), kind=kOutput, calls=%fused_computation.84 | convolution fusion | flops 539557888 | bytes 8389632 | tf_op jit(solution)/shard_map/dot_general | solution.py:192
  (184 shorter events, 77.0 us)
Async XLA Ops:
  0.0 7.6 %copy-start.3 = (bf16[128,4096]{1,0:T(8,128)(2,1)S(1)}, bf16[128,4096]{1,0:T(8,128)(2,1)}, u32[]{:S(2)}) copy-start(bf16[128,4096]{1,0:T(8,128)(2,1)} %param.19) | copy-start | bytes 3145732
  2.3 20.6 %all-to-all-start = ((bf16[128,8,512]{0,2,1:T(8,128)(2,1)}), bf16[128,8,512]{0,2,1:T(8,128)(2,1)S(1)}, u32[]{:S(2)}, u32[]{:S(2)}) async-start(bf16[128,8,512]{0,2,1:T(8,128)(2,1)} %bitcast.2), calls=%async_computation | async-start | bytes 2097152 | tf_op jit(solution)/shard_map/all_to_all | solution.py:102
  7.6 38.5 %copy-start.7 = (f32[8,128]{1,0:T(8,128)S(1)}, f32[8,128]{1,0:T(8,128)}, u32[]{:S(2)}) copy-start(f32[8,128]{1,0:T(8,128)} %param.21) | copy-start | bytes 12292
  7.6 57.0 %copy-start.8 = (f32[8,128]{1,0:T(8,128)S(1)}, f32[8,128]{1,0:T(8,128)}, u32[]{:S(2)}) copy-start(f32[8,128]{1,0:T(8,128)} %param.22) | copy-start | bytes 12292
  22.9 18.9 %all-to-all-start.1 = ((bf16[128,8,512]{0,2,1:T(8,128)(2,1)}), bf16[128,8,512]{0,2,1:T(8,128)(2,1)S(1)}, u32[]{:S(2)}, u32[]{:S(2)}) async-start(bf16[128,8,512]{0,2,1:T(8,128)(2,1)} %bitcast.5), calls=%async_computation.1 | async-start | bytes 2097152 | tf_op jit(solution)/shard_map/all_to_all | solution.py:103
  41.8 38.5 %all-to-all-start.2 = ((bf16[128,8,512]{0,2,1:T(8,128)(2,1)}), bf16[128,8,512]{0,2,1:T(8,128)(2,1)}, u32[]{:S(2)}, u32[]{:S(2)}) async-start(bf16[128,8,512]{0,2,1:T(8,128)(2,1)} %bitcast.8), calls=%async_computation.2 | async-start | bytes 2097152 | tf_op jit(solution)/shard_map/all_to_all | solution.py:101
  191.1 8.9 %copy-start.6 = (s32[128,2]{0,1:T(2,128)S(1)}, s32[128,2]{0,1:T(2,128)}, u32[]{:S(2)}) copy-start(s32[128,2]{0,1:T(2,128)} %param.28) | copy-start | bytes 3076
  196.2 30.2 %all-to-all-start.3 = ((f32[1024,1,512]{2,1,0:T(1,128)}), f32[1024,1,512]{2,1,0:T(1,128)S(1)}, u32[]{:S(2)}, u32[]{:S(2)}) async-start(f32[1024,1,512]{2,1,0:T(1,128)} %copy.92), calls=%async_computation.3 | async-start | bytes 4194304 | tf_op jit(solution)/shard_map/all_to_all | solution.py:146
  226.5 1.2 copy-start.2
  226.5 1.2 copy-start.4
  226.8 1.6 copy-start.5
  231.4 1.9 copy-start
  234.6 12.6 %collective-permute-start = (bf16[1,64,4096]{2,1,0:T(8,128)(2,1)}, bf16[1,64,4096]{2,1,0:T(8,128)(2,1)}, u32[]{:S(2)}, u32[]{:S(2)}) collective-permute-start(bf16[1,64,4096]{2,1,0:T(8,128)(2,1)} %get-tuple-element.181), channel_id=1, source_target_pairs={{0,28},{4,0},{8,4},{12,8},{16,12},{20,16},{24,20},{28,24},{1,29},{... | collective-permute-start | bytes 1572872 | tf_op jit(solution)/shard_map/ppermute | solution.py:177
  234.7 23.8 %collective-permute-start.1 = (bf16[1,64,4096]{2,1,0:T(8,128)(2,1)}, bf16[1,64,4096]{2,1,0:T(8,128)(2,1)}, u32[]{:S(2)}, u32[]{:S(2)}) collective-permute-start(bf16[1,64,4096]{2,1,0:T(8,128)(2,1)} %get-tuple-element.180), channel_id=1, source_target_pairs={{0,24},{4,28},{8,0},{12,4},{16,8},{20,12},{24,16},{28,20},{1,25},{... | collective-permute-start | bytes 1572872 | tf_op jit(solution)/shard_map/ppermute | solution.py:177
  235.2 25.2 %collective-permute-start.2 = (bf16[1,64,4096]{2,1,0:T(8,128)(2,1)}, bf16[1,64,4096]{2,1,0:T(8,128)(2,1)S(1)}, u32[]{:S(2)}, u32[]{:S(2)}) collective-permute-start(bf16[1,64,4096]{2,1,0:T(8,128)(2,1)} %get-tuple-element.179), channel_id=1, source_target_pairs={{0,20},{4,24},{8,28},{12,0},{16,4},{20,8},{24,12},{28,16},{1,21},{... | collective-permute-start | bytes 1572872 | tf_op jit(solution)/shard_map/ppermute | solution.py:177
  236.4 45.7 %collective-permute-start.3 = (bf16[1,64,4096]{2,1,0:T(8,128)(2,1)S(1)}, bf16[1,64,4096]{2,1,0:T(8,128)(2,1)S(1)}, u32[]{:S(2)}, u32[]{:S(2)}) collective-permute-start(bf16[1,64,4096]{2,1,0:T(8,128)(2,1)S(1)} %get-tuple-element.178), channel_id=1, source_target_pairs={{0,16},{4,20},{8,24},{12,28},{16,0},{20,4},{24,8},{28,12},{1,17},{... | collective-permute-start | bytes 1572872 | tf_op jit(solution)/shard_map/ppermute | solution.py:177
  237.1 46.7 %collective-permute-start.4 = (bf16[1,64,4096]{2,1,0:T(8,128)(2,1)S(1)}, bf16[1,64,4096]{2,1,0:T(8,128)(2,1)S(1)}, u32[]{:S(2)}, u32[]{:S(2)}) collective-permute-start(bf16[1,64,4096]{2,1,0:T(8,128)(2,1)S(1)} %get-tuple-element.177), channel_id=1, source_target_pairs={{0,12},{4,16},{8,20},{12,24},{16,28},{20,0},{24,4},{28,8},{1,13},{... | collective-permute-start | bytes 1572872 | tf_op jit(solution)/shard_map/ppermute | solution.py:177
  247.2 36.6 %collective-permute-start.5 = (bf16[1,64,4096]{2,1,0:T(8,128)(2,1)S(1)}, bf16[1,64,4096]{2,1,0:T(8,128)(2,1)S(1)}, u32[]{:S(2)}, u32[]{:S(2)}) collective-permute-start(bf16[1,64,4096]{2,1,0:T(8,128)(2,1)S(1)} %get-tuple-element.176), channel_id=1, source_target_pairs={{0,8},{4,12},{8,16},{12,20},{16,24},{20,28},{24,0},{28,4},{1,9},{5... | collective-permute-start | bytes 1572872 | tf_op jit(solution)/shard_map/ppermute | solution.py:177
  258.5 25.4 %collective-permute-start.6 = (bf16[1,64,4096]{2,1,0:T(8,128)(2,1)S(1)}, bf16[1,64,4096]{2,1,0:T(8,128)(2,1)S(1)}, u32[]{:S(2)}, u32[]{:S(2)}) collective-permute-start(bf16[1,64,4096]{2,1,0:T(8,128)(2,1)S(1)} %get-tuple-element.175), channel_id=1, source_target_pairs={{0,4},{4,8},{8,12},{12,16},{16,20},{20,24},{24,28},{28,0},{1,5},{5... | collective-permute-start | bytes 1572872 | tf_op jit(solution)/shard_map/ppermute | solution.py:177
  283.9 4.9 %slice-start = ((s8[5767168]{0:T(1024)(128)(4,1)}), s8[4194304]{0:T(1024)(128)(4,1)S(1)}, s32[]{:S(2)}) async-start(s8[5767168]{0:T(1024)(128)(4,1)} %bitcast.232), calls=%async_computation.5 | async-start | bytes 8388608
  285.2 3.6 slice-start.1
  286.8 2.0 copy-start.1
  306.0 4.7 %copy-start.9 = (f32[128,2]{0,1:T(2,128)S(1)}, f32[128,2]{0,1:T(2,128)}, u32[]{:S(2)}) copy-start(f32[128,2]{0,1:T(2,128)} %param.29) | copy-start | bytes 3076
  306.0 53.8 %all-to-all-start.4 = ((bf16[8,64,4096]{2,1,0:T(8,128)(2,1)}), bf16[8,64,4096]{2,1,0:T(8,128)(2,1)}, u32[]{:S(2)}, u32[]{:S(2)}) async-start(bf16[8,64,4096]{2,1,0:T(8,128)(2,1)} %bitcast.220), calls=%async_computation.4 | async-start | bytes 8388608 | tf_op jit(solution)/shard_map/all_to_all | solution.py:187
